TPU v7x, 256 devices: a whole 4x4x8 slice. The times are simulated.
256 devices in a mesh: rows: 32 (over x, z), cols: 8 (over y, core).
Axes of the slice: x: 4, y: 4, z: 8, core: 2. Of those that a mesh axis runs over, the one named last changes fastest.
Arguments:
- cube: float32 [1, 12288, 12288], P(None, 'rows', 'cols'), may hold values from -480 to 480
Outputs:
- scale_one: float32 [1, 12288, 12288], P(None, 'rows', 'cols')
- scale_two: float32 [1, 12288, 12288], P(None, 'rows', 'cols')
- scale_three: float32 [1, 12288, 12288], P(None, 'rows', 'cols')
- smooth: float32 [1, 12288, 12288], P(None, 'rows', 'cols')
- sigmas: float32 [3, 1], replicated
All inputs are finite; a program needn't handle non-finite values.
Results may differ from a plain program's by a relative error of at most 0.0002.
Values sent between devices are 32-bit elements; how exact they have to be, the bound alone decides.
A program may use at most 64 MiB of HBM per device.

v0:
```python
import jax
import jax.numpy as jnp
from jax import lax
from jax.sharding import Mesh
from jax.sharding import PartitionSpec as P

LEVELS = 3
ROWS = ("rows_0", "rows_1")
COLS = ("cols_0", "cols_1")
ROWS_COLS = ("rows_0", "rows_1", "cols_0", "cols_1")


def padded_2(array, sides, width):
    for axis, dim in sides:
        count, length = (lax.axis_size(axis), array.shape[dim])
        up = [(i, (i + 1) % count) for i in range(count - 1)]
        down = [(j, i) for i, j in up]
        last = lax.slice_in_dim(array, length - width, length, axis=dim)
        leading = lax.slice_in_dim(array, 0, width, axis=dim)
        before = lax.ppermute(last, axis, up)
        after = lax.ppermute(leading, axis, down)
        array = jnp.concatenate([before, array, after], axis=dim)
    return array


def one_axis_at_a_time(array, axes):
    for axis in axes:
        array = lax.psum(array, axis)
    return array


def filter_dim(x, dim, step):
    length = x.shape[dim]

    def part(lower, upper):
        return lax.slice_in_dim(x, lower, length - upper, axis=dim)

    outer = (part(0, 4 * step) + part(4 * step, 0)) * 0.0625
    inner = (part(step, 3 * step) + part(3 * step, step)) * 0.25
    return outer + inner + part(2 * step, 2 * step) * 0.375


def mirror_edges(padded, dim, width, position, extent):
    length = padded.shape[dim]
    upper_mirror = jnp.flip(lax.slice_in_dim(padded, width + 1, 2 * width + 1, axis=dim), dim)
    lower_mirror = jnp.flip(
        lax.slice_in_dim(padded, length - 2 * width - 1, length - width - 1, axis=dim), dim
    )
    upper_rim = lax.slice_in_dim(padded, 0, width, axis=dim)
    lower_rim = lax.slice_in_dim(padded, length - width, length, axis=dim)
    middle = lax.slice_in_dim(padded, width, length - width, axis=dim)
    upper_rim = jnp.where(position == 0, upper_mirror, upper_rim)
    lower_rim = jnp.where(position == extent - 1, lower_mirror, lower_rim)
    return jnp.concatenate([upper_rim, middle, lower_rim], axis=dim)


def crop_both(x, margin):
    if margin == 0:
        return x
    return x[:, margin:-margin, margin:-margin]


def on_device(cube):
    row_pos = lax.axis_index(ROWS)
    col_pos = lax.axis_index(COLS)
    row_count = lax.axis_size(ROWS)
    col_count = lax.axis_size(COLS)
    pixels = float(row_count * col_count * cube.shape[1] * cube.shape[2])
    planes = []
    squares = []

    def record(plane):
        square = jnp.sum(plane * plane, axis=(1, 2))
        squares.append(square)

    depth = 2 ** (LEVELS + 1) - 2
    padded = padded_2(cube, ((ROWS, 1), (COLS, 2)), depth)
    padded = mirror_edges(padded, 1, depth, row_pos, row_count)
    padded = mirror_edges(padded, 2, depth, col_pos, col_count)
    margin = depth
    for level in range(LEVELS):
        step = 2**level
        width = 2 * step
        nextsmooth = filter_dim(filter_dim(padded, 1, step), 2, step)
        plane = crop_both(padded, margin) - crop_both(nextsmooth, margin - width)
        planes.append(plane)
        record(plane)
        padded = nextsmooth
        margin = margin - width
    square_all = one_axis_at_a_time(jnp.stack(squares), ROWS_COLS)
    sigmas = jnp.sqrt(square_all / pixels + 1e-06)
    return (planes[0], planes[1], planes[2], padded, sigmas)


def solution(mesh):
    split = Mesh(mesh.devices.reshape(4, 8, 4, 2), ("rows_0", "rows_1", "cols_0", "cols_1"))
    return jax.shard_map(
        on_device,
        mesh=split,
        in_specs=(P(None, ROWS, COLS),),
        out_specs=(
            P(None, ROWS, COLS),
            P(None, ROWS, COLS),
            P(None, ROWS, COLS),
            P(None, ROWS, COLS),
            P(),
        ),
        check_vma=False,
    )
```

profile of v0, /device:TPU:1, one launch (start us, length us, event | category | flops | bytes accessed | tf_op | source)
XLA Modules:
  0.0 104.1 jit_solution(12735866396447164645)
XLA Ops:
  1.6 4.4 %collective-permute-start = (f32[1,14,1536]{2,1,0:T(8,128)S(1)}, f32[1,14,1536]{2,1,0:T(8,128)S(1)}, u32[]{:S(2)}, u32[]{:S(2)}) collective-permute-start(f32[1,14,1536]{2,1,0:T(8,128)S(1)} %get-tuple-element.28), channel_id=1, source_target_pairs={{0,8},{8,16},{16,24},{24,32},{32,40},{40,48},{48,56},{56,64},{64,7... | collective-permute-start | bytes 258056 | tf_op jit(solution)/shard_map/ppermute | solution.py:20
  6.0 1.3 %collective-permute-start.1 = (f32[1,14,1536]{2,1,0:T(8,128)S(1)}, f32[1,14,1536]{2,1,0:T(8,128)S(1)}, u32[]{:S(2)}, u32[]{:S(2)}) collective-permute-start(f32[1,14,1536]{2,1,0:T(8,128)S(1)} %get-tuple-element.29), channel_id=1, source_target_pairs={{8,0},{16,8},{24,16},{32,24},{40,32},{48,40},{56,48},{64,56},{72,6... | collective-permute-start | bytes 258056 | tf_op jit(solution)/shard_map/ppermute | solution.py:21
  7.6 3.9 %collective-permute-done.1 = f32[1,14,1536]{2,1,0:T(8,128)S(1)} collective-permute-done((f32[1,14,1536]{2,1,0:T(8,128)S(1)}, f32[1,14,1536]{2,1,0:T(8,128)S(1)}, u32[]{:S(2)}, u32[]{:S(2)}) %collective-permute-start.1) | collective-permute-done | bytes 86048 | tf_op jit(solution)/shard_map/ppermute | solution.py:21
  11.5 1.9 %pad_maximum_fusion.1 = f32[1,412,1536]{2,1,0:T(8,128)S(1)} fusion(f32[1,14,1536]{2,1,0:T(8,128)S(1)} %collective-permute-done.1, f32[1,384,1536]{2,1,0:T(8,128)} %param.1, f32[1,14,1536]{2,1,0:T(8,128)S(1)} %collective-permute-done), kind=kLoop, calls=%fused_computation.36 | loop fusion | flops 1265664 | bytes 5062656 | tf_op jit(solution)/shard_map/concatenate | solution.py:22
  13.6 3.8 %collective-permute-start.3 = (f32[1,412,14]{2,1,0:T(8,128)S(1)}, f32[1,412,14]{2,1,0:T(8,128)S(1)}, u32[]{:S(2)}, u32[]{:S(2)}) collective-permute-start(f32[1,412,14]{2,1,0:T(8,128)S(1)} %get-tuple-element.26), channel_id=1, source_target_pairs={{1,0},{2,1},{3,2},{4,3},{5,4},{6,5},{7,6},{9,8},{10,9},{11,10},{12... | collective-permute-start | bytes 69224 | tf_op jit(solution)/shard_map/ppermute | solution.py:21
  17.4 3.1 %collective-permute-start.2 = (f32[1,412,14]{2,1,0:T(8,128)S(1)}, f32[1,412,14]{2,1,0:T(8,128)S(1)}, u32[]{:S(2)}, u32[]{:S(2)}) collective-permute-start(f32[1,412,14]{2,1,0:T(8,128)S(1)} %get-tuple-element.27), channel_id=1, source_target_pairs={{0,1},{1,2},{2,3},{3,4},{4,5},{5,6},{6,7},{8,9},{9,10},{10,11},{11... | collective-permute-start | bytes 69224 | tf_op jit(solution)/shard_map/ppermute | solution.py:20
  20.6 1.6 %collective-permute-done.3 = f32[1,412,14]{2,1,0:T(8,128)S(1)} collective-permute-done((f32[1,412,14]{2,1,0:T(8,128)S(1)}, f32[1,412,14]{2,1,0:T(8,128)S(1)}, u32[]{:S(2)}, u32[]{:S(2)}) %collective-permute-start.3) | collective-permute-done | bytes 23104 | tf_op jit(solution)/shard_map/ppermute | solution.py:21
  22.1 1.2 %collective-permute-done.2 = f32[1,412,14]{2,1,0:T(8,128)S(1)} collective-permute-done((f32[1,412,14]{2,1,0:T(8,128)S(1)}, f32[1,412,14]{2,1,0:T(8,128)S(1)}, u32[]{:S(2)}, u32[]{:S(2)}) %collective-permute-start.2) | collective-permute-done | bytes 23104 | tf_op jit(solution)/shard_map/ppermute | solution.py:20
  23.3 2.7 %concatenate.13 = f32[1,412,1564]{2,1,0:T(8,128)} concatenate(f32[1,412,14]{2,1,0:T(8,128)S(1)} %collective-permute-done.2, f32[1,412,1536]{2,1,0:T(8,128)S(1)} %pad_maximum_fusion.1, f32[1,412,14]{2,1,0:T(8,128)S(1)} %collective-permute-done.3), dimensions={2} | concatenate | bytes 5154944 | tf_op jit(solution)/shard_map/concatenate | solution.py:22
  26.1 1.0 fusion.25
  27.1 1.9 %slice.195 = f32[1,384,1564]{2,1,0:T(8,128)S(1)} slice(f32[1,412,1564]{2,1,0:T(8,128)} %concatenate.13), slice={[0:1], [14:398], [0:1564]} | slice | bytes 4804608 | tf_op jit(solution)/shard_map/slice | solution.py:51
  30.8 1.8 %pad_maximum_fusion = f32[1,412,1564]{2,1,0:T(8,128)} fusion(f32[1,14,1564]{2,1,0:T(8,128)S(1)} %get-tuple-element.17, f32[1,384,1564]{2,1,0:T(8,128)S(1)} %slice.195, f32[1,14,1564]{2,1,0:T(8,128)S(1)} %get-tuple-element.16), kind=kLoop, calls=%fused_computation | loop fusion | flops 1288736 | bytes 5154944 | tf_op jit(solution)/shard_map/concatenate | solution.py:54
  33.6 4.0 %slice.198 = f32[1,412,1536]{2,1,0:T(8,128)} slice(f32[1,412,1564]{2,1,0:T(8,128)} %pad_maximum_fusion), slice={[0:1], [0:412], [14:1550]} | slice | bytes 5062656 | tf_op jit(solution)/shard_map/slice | solution.py:51
  38.4 3.2 %concatenate.15 = f32[1,412,1564]{2,1,0:T(8,128)S(1)} concatenate(f32[1,412,14]{2,1,0:T(8,128)} %get-tuple-element.13, f32[1,412,1536]{2,1,0:T(8,128)} %slice.198, f32[1,412,14]{2,1,0:T(8,128)S(1)} %get-tuple-element.12), dimensions={2} | concatenate | bytes 5154944 | tf_op jit(solution)/shard_map/concatenate | solution.py:54
  41.6 1.3 %fusion.4 = f32[1,408,1564]{2,1,0:T(8,128)S(1)} fusion(f32[1,412,1564]{2,1,0:T(8,128)S(1)} %concatenate.15), kind=kLoop, calls=%fused_computation.9 | loop fusion | flops 4466784 | bytes 15314688 | tf_op jit(solution)/shard_map/add | solution.py:40
  42.9 2.9 %fusion = f32[1,408,1560]{2,1,0:T(8,128)S(1)} fusion(f32[1,408,1564]{2,1,0:T(8,128)S(1)} %fusion.4), kind=kLoop, calls=%fused_computation.2 | loop fusion | flops 4455360 | bytes 15275520 | tf_op jit(solution)/shard_map/add | solution.py:40
  45.8 1.1 %fusion.12 = f32[1,400,1560]{2,1,0:T(8,128)S(1)} fusion(f32[1,408,1560]{2,1,0:T(8,128)S(1)} %fusion), kind=kLoop, calls=%fused_computation.23 | loop fusion | flops 4368000 | bytes 14976000 | tf_op jit(solution)/shard_map/add | solution.py:40
  46.9 2.8 %fusion.8 = f32[1,400,1552]{2,1,0:T(8,128)S(1)} fusion(f32[1,400,1560]{2,1,0:T(8,128)S(1)} %fusion.12), kind=kLoop, calls=%fused_computation.16 | loop fusion | flops 4345600 | bytes 14899200 | tf_op jit(solution)/shard_map/add | solution.py:40
  51.4 6.6 %multiply_reduce_fusion = (f32[]{:T(128)}, f32[1,384,1536]{2,1,0:T(8,128)}, f32[1,384,1536]{2,1,0:T(8,128)}, f32[]{:T(128)}, f32[1,384,1536]{2,1,0:T(8,128)}, /*index=5*/f32[]{:T(128)}, f32[1,384,1536]{2,1,0:T(8,128)}) fusion(f32[1,400,1552]{2,1,0:T(8,128)S(1)} %fusion.8, f32[1,384,1552]{2,1,0:T(8,128)S(1)} %fusion.16, f32[1,384,1536]{2,1,0:T(8,128)S(1)} %copy-done, ...), kind=kLoop, calls=%fused_computation.44 | loop fusion | flops 9437181 | bytes 28311564 | tf_op jit(solution)/shard_map/reduce_sum | solution.py:73
  57.9 2.0 %pad_maximum_fusion.4 = f32[3,1]{0,1:T(1,128)S(1)} fusion(f32[1,1]{0,1:T(1,128)} %bitcast.2, f32[1,1]{0,1:T(1,128)} %bitcast.1, f32[1,1]{0,1:T(1,128)} %bitcast), kind=kLoop, calls=%fused_computation.56 | loop fusion | flops 6 | bytes 24 | tf_op jit(solution)/shard_map/stack | solution.py:90
  59.9 10.3 %psum.28 = f32[3,1]{0,1:T(1,128)S(1)} all-reduce(f32[3,1]{0,1:T(1,128)S(1)} %pad_maximum_fusion.4), channel_id=1, replica_groups=mesh['rows_0'=4,'rows_1'=8,'cols_0'=4,'cols_1'=2] {'rows_0'}, use_global_device_ids=true, to_apply=%region_3.4 | all-reduce | flops 3 | bytes 24 | tf_op jit(solution)/shard_map/psum | solution.py:28
  70.2 13.5 %psum.29 = f32[3,1]{0,1:T(1,128)S(1)} all-reduce(f32[3,1]{0,1:T(1,128)S(1)} %psum.28), channel_id=1, replica_groups=mesh['rows_0'=4,'rows_1'=8,'cols_0'=4,'cols_1'=2] {'rows_1'}, use_global_device_ids=true, to_apply=%region_4.5 | all-reduce | flops 3 | bytes 24 | tf_op jit(solution)/shard_map/psum | solution.py:28
  83.7 7.4 %psum.30 = f32[3,1]{0,1:T(1,128)S(1)} all-reduce(f32[3,1]{0,1:T(1,128)S(1)} %psum.29), channel_id=1, replica_groups=mesh['rows_0'=4,'rows_1'=8,'cols_0'=4,'cols_1'=2] {'cols_0'}, use_global_device_ids=true, to_apply=%region_5.6 | all-reduce | flops 3 | bytes 24 | tf_op jit(solution)/shard_map/psum | solution.py:28
  91.1 12.5 %psum.31 = f32[3,1]{0,1:T(1,128)S(1)} all-reduce(f32[3,1]{0,1:T(1,128)S(1)} %psum.30), channel_id=1, replica_groups=mesh['rows_0'=4,'rows_1'=8,'cols_0'=4,'cols_1'=2] {'cols_1'}, use_global_device_ids=true, to_apply=%region_6.7 | all-reduce | flops 3 | bytes 24 | tf_op jit(solution)/shard_map/psum | solution.py:28
  (14 shorter events, 7.2 us)
Async XLA Ops:
  1.6 6.0 %collective-permute-start = (f32[1,14,1536]{2,1,0:T(8,128)S(1)}, f32[1,14,1536]{2,1,0:T(8,128)S(1)}, u32[]{:S(2)}, u32[]{:S(2)}) collective-permute-start(f32[1,14,1536]{2,1,0:T(8,128)S(1)} %get-tuple-element.28), channel_id=1, source_target_pairs={{0,8},{8,16},{16,24},{24,32},{32,40},{40,48},{48,56},{56,64},{64,7... | collective-permute-start | bytes 258056 | tf_op jit(solution)/shard_map/ppermute | solution.py:20
  6.0 5.5 %collective-permute-start.1 = (f32[1,14,1536]{2,1,0:T(8,128)S(1)}, f32[1,14,1536]{2,1,0:T(8,128)S(1)}, u32[]{:S(2)}, u32[]{:S(2)}) collective-permute-start(f32[1,14,1536]{2,1,0:T(8,128)S(1)} %get-tuple-element.29), channel_id=1, source_target_pairs={{8,0},{16,8},{24,16},{32,24},{40,32},{48,40},{56,48},{64,56},{72,6... | collective-permute-start | bytes 258056 | tf_op jit(solution)/shard_map/ppermute | solution.py:21
  13.6 8.5 %collective-permute-start.3 = (f32[1,412,14]{2,1,0:T(8,128)S(1)}, f32[1,412,14]{2,1,0:T(8,128)S(1)}, u32[]{:S(2)}, u32[]{:S(2)}) collective-permute-start(f32[1,412,14]{2,1,0:T(8,128)S(1)} %get-tuple-element.26), channel_id=1, source_target_pairs={{1,0},{2,1},{3,2},{4,3},{5,4},{6,5},{7,6},{9,8},{10,9},{11,10},{12... | collective-permute-start | bytes 69224 | tf_op jit(solution)/shard_map/ppermute | solution.py:21
  17.4 5.9 %collective-permute-start.2 = (f32[1,412,14]{2,1,0:T(8,128)S(1)}, f32[1,412,14]{2,1,0:T(8,128)S(1)}, u32[]{:S(2)}, u32[]{:S(2)}) collective-permute-start(f32[1,412,14]{2,1,0:T(8,128)S(1)} %get-tuple-element.27), channel_id=1, source_target_pairs={{0,1},{1,2},{2,3},{3,4},{4,5},{5,6},{6,7},{8,9},{9,10},{10,11},{11... | collective-permute-start | bytes 69224 | tf_op jit(solution)/shard_map/ppermute | solution.py:20
  49.7 1.7 %copy-start = (f32[1,384,1536]{2,1,0:T(8,128)S(1)}, f32[1,384,1536]{2,1,0:T(8,128)}, u32[]{:S(2)}) copy-start(f32[1,384,1536]{2,1,0:T(8,128)} %param.1) | copy-start | bytes 7077892
where the time goes:
time: 105 us; the launch traced here: 104 us
  blocking collectives  43.7 us (42%)
  other arithmetic  23.5 us (22%)
  local copies, waits for them, and re-layouts  16.5 us (16%)
  starting transfers between devices  12.6 us (12%)
  waiting for transfers between devices  6.99 us (7%)
    psum x4, blocking collectives, one_axis_at_a_time(): array = lax.psum(array, axis)  43.7 us
    add x5, other arithmetic, filter_dim(): return outer + inner + part(2 * step, 2 * step) * 0.375  8.84 us
    ppermute x2, starting transfers between devices, padded_2(): before = lax.ppermute(last, axis, up)  7.47 us
    reduce_sum x1, other arithmetic, record(): square = jnp.sum(plane * plane, axis=(1, 2))  6.58 us
    slice x2, local copies, waits for them, and re-layouts, mirror_edges(): middle = lax.slice_in_dim(padded, width, length - width, axis=dim)  5.9 us
    ppermute x2, waiting for transfers between devices, padded_2(): after = lax.ppermute(leading, axis, down)  5.5 us
    ppermute x2, starting transfers between devices, padded_2(): after = lax.ppermute(leading, axis, down)  5.12 us
    concatenate x1, local copies, waits for them, and re-layouts, mirror_edges(): return jnp.concatenate([upper_rim, middle, lower_rim], axis=dim)  3.22 us
  transfers between devices with their start and end apart: 4, of which 4 were waited for; matrix products, arithmetic and copies ran while one was open for 0% of the time, Pallas kernels for 0%

commit v1 on v0

v1 whole, which is shorter than its diff:
```python
import functools

import jax
import jax.numpy as jnp
from jax import lax
from jax.experimental import pallas as pl
from jax.experimental.pallas import tpu as pltpu
from jax.sharding import PartitionSpec as P

MESH = pl.DeviceIdType.MESH
F32 = jnp.float32

NROW, NCOL = 32, 8
NX, NZ = 4, 8
R, C = 384, 1536
NCH = C // 128
HALO = NCH
OFF = 24
TOP, BOT = OFF, OFF + R
ROWS = R + 2 * OFF
EDGE = 16
PIXELS = float(NROW * NCOL * R * C)


def row_pass(src, c, r, h):
    def at(k):
        return src[c, pl.ds(r + k, 8), :]

    return (at(-2 * h) + at(2 * h)) + (at(-h) + at(h)) * 4.0 + at(0) * 6.0


def stage(src, dst, shift, h, first, last, outs, plane=None, plane_chunks=()):
    lane = lax.broadcasted_iota(jnp.int32, (8, 128), 1)
    lo1, lo2 = lane < h, lane < 2 * h
    hi1, hi2 = lane >= 128 - h, lane >= 128 - 2 * h
    needed = []
    for c in outs:
        for k in ((c - 1) % (NCH + 1), c, (c + 1) % (NCH + 1)):
            if k not in needed:
                needed.append(k)

    def block(i, acc):
        r = pl.multiple_of(first + 8 * i, 8)
        v, rolled = {}, {}
        for c in needed:
            v[c] = row_pass(src, c, r, h)

        def roll(c, s):
            if (c, s) not in rolled:
                rolled[c, s] = pltpu.roll(v[c], s % 128, 1)
            return rolled[c, s]

        for c in outs:
            p, n = (c - 1) % (NCH + 1), (c + 1) % (NCH + 1)
            left1 = jnp.where(lo1, roll(p, h), roll(c, h))
            right1 = jnp.where(hi1, roll(n, -h), roll(c, -h))
            left2 = jnp.where(lo2, roll(p, 2 * h), roll(c, 2 * h))
            right2 = jnp.where(hi2, roll(n, -2 * h), roll(c, -2 * h))
            out = (
                (left2 + right2) * (1.0 / 256)
                + (left1 + right1) * (4.0 / 256)
                + v[c] * (6.0 / 256)
            )
            if shift == 0 or c in plane_chunks:
                dst[c, pl.ds(pl.multiple_of(r - shift, 8), 8), :] = out
            if c in plane_chunks:
                w = src[c, pl.ds(r, 8), :] - out
                plane[c, pl.ds(pl.multiple_of(r - OFF, 8), 8), :] = w
                acc = acc + w * w
        return acc

    return lax.fori_loop(0, (last - first) // 8, block, jnp.zeros((8, 128), F32))


def kernel_main(
    cube, w1, w2, w3, smooth, sigma,
    c0, c1, c2, from_left, from_right, mine, mine2, plane_sums, line_sums,
    load_sem, send_sem, recv_sem, sum_send, sum_recv,
):
    row, col = lax.axis_index("rows"), lax.axis_index("cols")
    x, z = row // NZ, row % NZ
    up, down = row > 0, row < NROW - 1
    left, right = col > 0, col < NCOL - 1
    me_plane = x * NCOL + col

    def both(a, b):
        return jnp.logical_and(a, b)

    everything = pl.ds(0, NCH)
    top_own, bottom_own = pl.ds(TOP, EDGE), pl.ds(BOT - EDGE, EDGE)
    above, below = pl.ds(TOP - EDGE, EDGE), pl.ds(BOT, EDGE)
    own = pl.ds(TOP, R)
    halos = [
        (left, 0, -1, c0.at[0, own], from_right.at[own]),
        (right, 0, 1, c0.at[NCH - 1, own], from_left.at[own]),
        (up, -1, 0, c0.at[everything, top_own], c0.at[everything, below]),
        (down, 1, 0, c0.at[everything, bottom_own], c0.at[everything, above]),
        (both(up, left), -1, -1, c0.at[0, top_own], from_right.at[below]),
        (both(up, right), -1, 1, c0.at[NCH - 1, top_own], from_left.at[below]),
        (both(down, left), 1, -1, c0.at[0, bottom_own], from_right.at[above]),
        (both(down, right), 1, 1, c0.at[NCH - 1, bottom_own], from_left.at[above]),
    ]

    def halo_copy(k):
        _, dr, dc, src, dst = halos[k]
        return pltpu.make_async_remote_copy(
            src_ref=src, dst_ref=dst, send_sem=send_sem.at[k], recv_sem=recv_sem.at[k],
            device_id=(row + dr, col + dc), device_id_type=MESH,
        )

    def load(c, part):
        a, n = ((0, EDGE), (R - EDGE, EDGE), (EDGE, R - 2 * EDGE))[part]
        return pltpu.make_async_copy(
            cube.at[0, pl.ds(a, n), pl.ds(c * 128, 128)],
            c0.at[c, pl.ds(TOP + a, n)],
            load_sem.at[c, part],
        )

    order = [0, NCH - 1] + list(range(1, NCH - 1))
    for c in order:
        load(c, 0).start()
        load(c, 1).start()
    for c in order:
        load(c, 2).start()

    barrier = pltpu.get_barrier_semaphore()
    count = jnp.int32(NX * NCOL - 1 + NZ - 1)
    for exists, dr, dc, _, _ in halos:
        count = count + exists.astype(jnp.int32)

        @pl.when(exists)
        def _():
            pl.semaphore_signal(barrier, inc=1, device_id=(row + dr, col + dc), device_id_type=MESH)

    def plane_peer(k):
        other = (me_plane + k) % (NX * NCOL)
        return ((other // NCOL) * NZ + z, other % NCOL)

    def line_peer(k):
        return (x * NZ + (z + k) % NZ, col)

    for k in range(1, NX * NCOL):
        pl.semaphore_signal(barrier, inc=1, device_id=plane_peer(k), device_id_type=MESH)
    for k in range(1, NZ):
        pl.semaphore_signal(barrier, inc=1, device_id=line_peer(k), device_id_type=MESH)

    for c in order:
        load(c, 0).wait()
        load(c, 1).wait()
    load(0, 2).wait()
    load(NCH - 1, 2).wait()
    pl.semaphore_wait(barrier, count)
    for k in range(8):
        @pl.when(halos[k][0])
        def _():
            halo_copy(k).start()
    for c in order[2:]:
        load(c, 2).wait()

    inner = tuple(range(1, NCH - 1))
    whole = tuple(range(NCH))
    rim = (NCH - 1, HALO, 0)
    rim_own = (NCH - 1, 0)

    a1 = stage(c0, c1, 0, 1, TOP + 8, BOT - 8, whole, w1, inner)
    a2 = stage(c1, c2, 0, 2, TOP + 16, BOT - 16, whole, w2, inner)
    a3 = stage(c2, smooth, OFF, 4, TOP + 24, BOT - 24, inner, w3, inner)

    for k in range(8):
        _, dr, dc, _, _ = halos[k]
        arrives = {0: right, 1: left, 2: down, 3: up,
                   4: both(down, right), 5: both(down, left),
                   6: both(up, right), 7: both(up, left)}[k]

        @pl.when(arrives)
        def _():
            halo_copy(k).wait_recv()

    lane = lax.broadcasted_iota(jnp.int32, (8, 128), 1)
    src_lane = lax.broadcasted_iota(jnp.int32, (128, 128), 0)
    dst_lane = lax.broadcasted_iota(jnp.int32, (128, 128), 1)

    def mirrored(chunk, total, dst):
        turn = (src_lane + dst_lane == total).astype(F32)
        dst[pl.ds(8, ROWS - 16), :] = lax.dot_general(
            c0[chunk, pl.ds(8, ROWS - 16), :], turn, (((1,), (0,)), ((), ())),
            precision=lax.Precision.HIGHEST, preferred_element_type=F32,
        )

    @pl.when(jnp.logical_not(left))
    def _():
        mirrored(0, 128, from_left)

    @pl.when(jnp.logical_not(right))
    def _():
        mirrored(NCH - 1, 126, from_right)

    def merge(i, carry):
        r = pl.multiple_of(8 + 8 * i, 8)
        c0[HALO, pl.ds(r, 8), :] = jnp.where(
            lane < 64, from_right[pl.ds(r, 8), :], from_left[pl.ds(r, 8), :]
        )
        return carry

    lax.fori_loop(0, (ROWS - 16) // 8, merge, 0)

    @pl.when(jnp.logical_not(up))
    def _():
        for i in range(1, 15):
            c0[:, pl.ds(TOP - i, 1), :] = c0[:, pl.ds(TOP + i, 1), :]

    @pl.when(jnp.logical_not(down))
    def _():
        for i in range(1, 15):
            c0[:, pl.ds(BOT - 1 + i, 1), :] = c0[:, pl.ds(BOT - 1 - i, 1), :]

    every = tuple(range(NCH + 1))
    a1 += stage(c0, c1, 0, 1, TOP + 8, BOT - 8, rim, w1, rim_own)
    a2 += stage(c1, c2, 0, 2, TOP + 16, BOT - 16, rim, w2, rim_own)
    a3 += stage(c2, smooth, OFF, 4, TOP + 24, BOT - 24, rim_own, w3, rim_own)
    stage(c0, c1, 0, 1, TOP - 16, TOP, every)
    stage(c0, c1, 0, 1, BOT, BOT + 16, every)
    a1 += stage(c0, c1, 0, 1, TOP, TOP + 8, every, w1, whole)
    a1 += stage(c0, c1, 0, 1, BOT - 8, BOT, every, w1, whole)
    stage(c1, c2, 0, 2, TOP - 8, TOP, every)
    stage(c1, c2, 0, 2, BOT, BOT + 8, every)
    a2 += stage(c1, c2, 0, 2, TOP, TOP + 16, every, w2, whole)
    a2 += stage(c1, c2, 0, 2, BOT - 16, BOT, every, w2, whole)
    a3 += stage(c2, smooth, OFF, 4, TOP, TOP + 24, whole, w3, whole)
    a3 += stage(c2, smooth, OFF, 4, BOT - 24, BOT, whole, w3, whole)

    lane1 = lax.broadcasted_iota(jnp.int32, (1, 128), 1)

    def total(a):
        return jnp.sum(jnp.sum(a, axis=0, keepdims=True), axis=1, keepdims=True)

    vec = jnp.where(lane1 == 0, total(a1), jnp.where(lane1 == 1, total(a2), total(a3)))

    def gather(value, own_ref, slots, index, count, peer, which):
        own_ref[...] = value
        slots[pl.ds(index, 1)] = value[None]
        for k in range(1, count):
            pltpu.make_async_remote_copy(
                src_ref=own_ref, dst_ref=slots.at[index],
                send_sem=sum_send.at[which], recv_sem=sum_recv.at[which],
                device_id=peer(k), device_id_type=MESH,
            ).start()
        arrived = slots.at[pl.ds(0, count - 1)]
        pltpu.make_async_copy(arrived, arrived, sum_recv.at[which]).wait()
        return jnp.sum(slots[...], axis=0)

    vec = gather(vec, mine, plane_sums, me_plane, NX * NCOL, plane_peer, 0)
    vec = gather(vec, mine2, line_sums, z, NZ, line_peer, 1)
    sigma[...] = jnp.sqrt(vec * (1.0 / PIXELS) + 1e-6)

    for which, slots, count in ((0, plane_sums, NX * NCOL), (1, line_sums, NZ)):
        sent = slots.at[pl.ds(0, count - 1)]
        pltpu.make_async_copy(sent, sent, sum_send.at[which]).wait()
    for k in range(8):
        @pl.when(halos[k][0])
        def _():
            halo_copy(k).wait_send()


def kernel_write(w1, w2, w3, smooth, sigma, o1, o2, o3, o4, o5, sem):
    pairs = ((w1, o1), (w2, o2), (w3, o3), (smooth, o4))
    for i, (a, o) in enumerate(pairs):
        for c in range(NCH):
            pltpu.make_async_copy(
                a.at[c], o.at[0, :, pl.ds(c * 128, 128)], sem.at[i]
            ).start()
    o5[...] = sigma[:, :3]
    for i, (a, o) in enumerate(pairs):
        pltpu.make_async_copy(a, a, sem.at[i]).wait()


def on_device(cube):
    vmem = pl.BlockSpec(memory_space=pltpu.VMEM)
    hbm = pl.BlockSpec(memory_space=pltpu.HBM)
    block = jax.ShapeDtypeStruct((NCH, R, 128), F32)
    cube = pltpu.with_memory_space_constraint(cube, pltpu.HBM)
    planes = pl.pallas_call(
        kernel_main,
        out_shape=[block] * 4 + [jax.ShapeDtypeStruct((1, 128), F32)],
        in_specs=[hbm],
        out_specs=[vmem] * 5,
        scratch_shapes=[
            pltpu.VMEM((NCH + 1, ROWS, 128), F32),
            pltpu.VMEM((NCH + 1, ROWS, 128), F32),
            pltpu.VMEM((NCH + 1, ROWS, 128), F32),
            pltpu.VMEM((ROWS, 128), F32),
            pltpu.VMEM((ROWS, 128), F32),
            pltpu.VMEM((1, 128), F32),
            pltpu.VMEM((1, 128), F32),
            pltpu.VMEM((NX * NCOL, 1, 128), F32),
            pltpu.VMEM((NZ, 1, 128), F32),
            pltpu.SemaphoreType.DMA((NCH, 3)),
            pltpu.SemaphoreType.DMA((8,)),
            pltpu.SemaphoreType.DMA((8,)),
            pltpu.SemaphoreType.DMA((2,)),
            pltpu.SemaphoreType.DMA((2,)),
        ],
        compiler_params=pltpu.CompilerParams(
            collective_id=0, has_side_effects=True, vmem_limit_bytes=40 * 2**20
        ),
        name="starlet",
    )(cube)
    out = jax.ShapeDtypeStruct((1, R, C), F32)
    o = pl.pallas_call(
        kernel_write,
        out_shape=[out] * 4 + [jax.ShapeDtypeStruct((1, 3), F32)],
        in_specs=[vmem] * 5,
        out_specs=[hbm] * 4 + [vmem],
        scratch_shapes=[pltpu.SemaphoreType.DMA((4,))],
        compiler_params=pltpu.CompilerParams(vmem_limit_bytes=16 * 2**20),
        name="write",
    )(*planes)
    return o[0], o[1], o[2], o[3], o[4].T


def solution(mesh):
    block = P(None, "rows", "cols")
    return jax.shard_map(
        on_device,
        mesh=mesh,
        in_specs=(block,),
        out_specs=(block,) * 4 + (P(),),
        check_vma=False,
    )
```

time: 105 us -> 57.2 us (0.54)
  Pallas kernels: 0 us -> 56.5 us
  blocking collectives: 43.7 us -> 0 us
  other arithmetic: 23.5 us -> 0 us
  local copies, waits for them, and re-layouts: 16.5 us -> 0 us
  starting transfers between devices: 12.6 us -> 0 us
  waiting for transfers between devices: 6.99 us -> 0 us
    pallas_call x0 -> x2, Pallas kernels: none -> 56.5 us  [the longest x1 52.4 us: on_device(): pl.pallas_call(kernel_main, out_shape=[block] * 4 + [jax.ShapeDtypeStruct...]
    psum x4 -> x0, blocking collectives: 43.7 us -> none  [one_axis_at_a_time(): array = lax.psum(array, axis)]
    ppermute x4 -> x0, starting transfers between devices: 12.6 us -> none  [the longest x2 7.47 us: padded_2(): before = lax.ppermute(last, axis, up)]
    add x5 -> x0, other arithmetic: 8.84 us -> none  [filter_dim(): return outer + inner + part(2 * step, 2 * step) * 0.375]
    slice x5 -> x0, local copies, waits for them, and re-layouts: 7.99 us -> none  [the longest x2 5.9 us: mirror_edges(): middle = lax.slice_in_dim(padded, width, length - width, axis=dim)]
    ppermute x4 -> x0, waiting for transfers between devices: 6.99 us -> none  [the longest x2 5.5 us: padded_2(): after = lax.ppermute(leading, axis, down)]
    reduce_sum x1 -> x0, other arithmetic: 6.58 us -> none  [record(): square = jnp.sum(plane * plane, axis=(1, 2))]
    concatenate x2 -> x0, local copies, waits for them, and re-layouts: 5.96 us -> none  [the longest x1 3.22 us: mirror_edges(): return jnp.concatenate([upper_rim, middle, lower_rim], axis=dim)]
  transfers between devices with their start and end apart: 4 -> 0, of which waited for: 4 -> 0; matrix products, arithmetic and copies ran while one was open for 0% -> 0% of each run, Pallas kernels for 0% -> 0%
where the time goes in v1:
time: 57.2 us; the launch traced here: 57.1 us
  Pallas kernels  56.5 us (99%)
  between operations  0.64 us (1%)
    pallas_call x1, Pallas kernels, on_device(): pl.pallas_call(kernel_main, out_shape=[block] * 4 + [jax.ShapeDtypeStruct...  52.4 us
    pallas_call x1, Pallas kernels, on_device(): pl.pallas_call(kernel_write, out_shape=[out] * 4 + [jax.ShapeDtypeStruct(...  4.11 us

profile of v1, /device:TPU:1, one launch (start us, length us, event | category | flops | bytes accessed | tf_op | source)
XLA Modules:
  0.0 57.1 jit_solution(11547644110582104386)
XLA Ops:
  0.6 52.4 %starlet.1 = (f32[12,384,128]{2,1,0:T(8,128)S(1)}, f32[12,384,128]{2,1,0:T(8,128)S(1)}, f32[12,384,128]{2,1,0:T(8,128)S(1)}, f32[12,384,128]{2,1,0:T(8,128)S(1)}, f32[1,128]{1,0:T(1,128)S(1)}) custom-call(f32[1,384,1536]{2,1,0:T(8,128)} %cube.1), custom_call_target="tpu_custom_call" | custom-call | tf_op jit(solution)/shard_map/starlet/pallas_call | solution.py:282
  53.0 4.1 %write.1 = (f32[1,384,1536]{2,1,0:T(8,128)}, f32[1,384,1536]{2,1,0:T(8,128)}, f32[1,384,1536]{2,1,0:T(8,128)}, f32[1,384,1536]{2,1,0:T(8,128)}, f32[1,3]{1,0:T(1,128)}) custom-call(f32[12,384,128]{2,1,0:T(8,128)S(1)} %get-tuple-element.15.w1, f32[12,384,128]{2,1,0:T(8,128)S(1)} %get-tuple-element.16.w2, f32[12,384,128]{2,1,0:T(8,128)S(1)} %get-tuple-element.17.w3, ...), custom_call_target="tpu_custom_call" | custom-call | tf_op jit(solution)/shard_map/write/pallas_call | solution.py:309

commit v2 on v1

--- a/solution.py
+++ b/solution.py
@@ -26,21 +26,18 @@
     def at(k):
         return src[c, pl.ds(r + k, 8), :]
 
-    return (at(-2 * h) + at(2 * h)) + (at(-h) + at(h)) * 4.0 + at(0) * 6.0
-
-
-def stage(src, dst, shift, h, first, last, outs, plane=None, plane_chunks=()):
+    ends = (at(-2 * h) + at(2 * h)) * (1.0 / 256)
+    return ends + (at(-h) + at(h)) * (4.0 / 256) + at(0) * (6.0 / 256)
+
+
+def stage(src, dst, shift, h, rows, outs, plane=None, plane_chunks=()):
     lane = lax.broadcasted_iota(jnp.int32, (8, 128), 1)
     lo1, lo2 = lane < h, lane < 2 * h
     hi1, hi2 = lane >= 128 - h, lane >= 128 - 2 * h
-    needed = []
-    for c in outs:
-        for k in ((c - 1) % (NCH + 1), c, (c + 1) % (NCH + 1)):
-            if k not in needed:
-                needed.append(k)
-
-    def block(i, acc):
-        r = pl.multiple_of(first + 8 * i, 8)
+    ring = NCH + 1
+    needed = list(dict.fromkeys(k for c in outs for k in ((c - 1) % ring, c, (c + 1) % ring)))
+
+    def block(r, inside, acc):
         v, rolled = {}, {}
         for c in needed:
             v[c] = row_pass(src, c, r, h)
@@ -51,25 +48,34 @@
             return rolled[c, s]
 
         for c in outs:
-            p, n = (c - 1) % (NCH + 1), (c + 1) % (NCH + 1)
+            p, n = (c - 1) % ring, (c + 1) % ring
             left1 = jnp.where(lo1, roll(p, h), roll(c, h))
             right1 = jnp.where(hi1, roll(n, -h), roll(c, -h))
             left2 = jnp.where(lo2, roll(p, 2 * h), roll(c, 2 * h))
             right2 = jnp.where(hi2, roll(n, -2 * h), roll(c, -2 * h))
-            out = (
-                (left2 + right2) * (1.0 / 256)
-                + (left1 + right1) * (4.0 / 256)
-                + v[c] * (6.0 / 256)
-            )
+            out = (left2 + right2) + (left1 + right1) * 4.0 + v[c] * 6.0
             if shift == 0 or c in plane_chunks:
-                dst[c, pl.ds(pl.multiple_of(r - shift, 8), 8), :] = out
-            if c in plane_chunks:
+                dst[c, pl.ds(r - shift, 8), :] = out
+            if inside and c in plane_chunks:
                 w = src[c, pl.ds(r, 8), :] - out
-                plane[c, pl.ds(pl.multiple_of(r - OFF, 8), 8), :] = w
+                plane[c, pl.ds(r - OFF, 8), :] = w
                 acc = acc + w * w
         return acc
 
-    return lax.fori_loop(0, (last - first) // 8, block, jnp.zeros((8, 128), F32))
+    acc = jnp.zeros((8, 128), F32)
+    if isinstance(rows, list):
+        for r in rows:
+            acc = block(r, TOP <= r < BOT, acc)
+        return acc
+    n = len(rows)
+    u = next(q for q in (6, 4, 3, 2, 1) if n % q == 0)
+
+    def several(i, acc):
+        for j in range(u):
+            acc = block(pl.multiple_of(rows[0] + 8 * (i * u + j), 8), True, acc)
+        return acc
+
+    return lax.fori_loop(0, n // u, several, acc)
 
 
 def kernel_main(
@@ -162,9 +168,10 @@
     rim = (NCH - 1, HALO, 0)
     rim_own = (NCH - 1, 0)
 
-    a1 = stage(c0, c1, 0, 1, TOP + 8, BOT - 8, whole, w1, inner)
-    a2 = stage(c1, c2, 0, 2, TOP + 16, BOT - 16, whole, w2, inner)
-    a3 = stage(c2, smooth, OFF, 4, TOP + 24, BOT - 24, inner, w3, inner)
+    mid1, mid2, mid3 = (range(TOP + k, BOT - k, 8) for k in (8, 16, 24))
+    a1 = stage(c0, c1, 0, 1, mid1, whole, w1, inner)
+    a2 = stage(c1, c2, 0, 2, mid2, whole, w2, inner)
+    a3 = stage(c2, smooth, OFF, 4, mid3, inner, w3, inner)
 
     for k in range(8):
         _, dr, dc, _, _ = halos[k]
@@ -215,19 +222,16 @@
             c0[:, pl.ds(BOT - 1 + i, 1), :] = c0[:, pl.ds(BOT - 1 - i, 1), :]
 
     every = tuple(range(NCH + 1))
-    a1 += stage(c0, c1, 0, 1, TOP + 8, BOT - 8, rim, w1, rim_own)
-    a2 += stage(c1, c2, 0, 2, TOP + 16, BOT - 16, rim, w2, rim_own)
-    a3 += stage(c2, smooth, OFF, 4, TOP + 24, BOT - 24, rim_own, w3, rim_own)
-    stage(c0, c1, 0, 1, TOP - 16, TOP, every)
-    stage(c0, c1, 0, 1, BOT, BOT + 16, every)
-    a1 += stage(c0, c1, 0, 1, TOP, TOP + 8, every, w1, whole)
-    a1 += stage(c0, c1, 0, 1, BOT - 8, BOT, every, w1, whole)
-    stage(c1, c2, 0, 2, TOP - 8, TOP, every)
-    stage(c1, c2, 0, 2, BOT, BOT + 8, every)
-    a2 += stage(c1, c2, 0, 2, TOP, TOP + 16, every, w2, whole)
-    a2 += stage(c1, c2, 0, 2, BOT - 16, BOT, every, w2, whole)
-    a3 += stage(c2, smooth, OFF, 4, TOP, TOP + 24, whole, w3, whole)
-    a3 += stage(c2, smooth, OFF, 4, BOT - 24, BOT, whole, w3, whole)
+    a1 += stage(c0, c1, 0, 1, mid1, rim, w1, rim_own)
+    a2 += stage(c1, c2, 0, 2, mid2, rim, w2, rim_own)
+    a3 += stage(c2, smooth, OFF, 4, mid3, rim_own, w3, rim_own)
+
+    def ends(a, b):
+        return list(range(TOP + a, TOP + b, 8)) + list(range(BOT - b, BOT - a, 8))
+
+    a1 += stage(c0, c1, 0, 1, ends(-16, 8), every, w1, whole)
+    a2 += stage(c1, c2, 0, 2, ends(-8, 16), every, w2, whole)
+    a3 += stage(c2, smooth, OFF, 4, ends(0, 24), whole, w3, whole)
 
     lane1 = lax.broadcasted_iota(jnp.int32, (1, 128), 1)
 

time: 57.2 us -> 41.3 us (0.72)
  Pallas kernels: 56.5 us -> 40.6 us
    pallas_call x1, Pallas kernels: 52.4 us -> 36.5 us  [on_device(): pl.pallas_call(kernel_main, out_shape=[block] * 4 + [jax.ShapeDtypeStruct...]
where the time goes in v2:
time: 41.3 us; the launch traced here: 41.2 us
  Pallas kernels  40.6 us (98%)
  between operations  0.64 us (2%)
    pallas_call x1, Pallas kernels, on_device(): pl.pallas_call(kernel_main, out_shape=[block] * 4 + [jax.ShapeDtypeStruct...  36.5 us
    pallas_call x1, Pallas kernels, on_device(): pl.pallas_call(kernel_write, out_shape=[out] * 4 + [jax.ShapeDtypeStruct(...  4.11 us

profile of v2, /device:TPU:1, one launch (start us, length us, event | category | flops | bytes accessed | tf_op | source)
XLA Modules:
  0.0 41.2 jit_solution(14153558912029954885)
XLA Ops:
  0.6 36.5 %starlet.1 = (f32[12,384,128]{2,1,0:T(8,128)S(1)}, f32[12,384,128]{2,1,0:T(8,128)S(1)}, f32[12,384,128]{2,1,0:T(8,128)S(1)}, f32[12,384,128]{2,1,0:T(8,128)S(1)}, f32[1,128]{1,0:T(1,128)S(1)}) custom-call(f32[1,384,1536]{2,1,0:T(8,128)} %cube.1), custom_call_target="tpu_custom_call" | custom-call | tf_op jit(solution)/shard_map/starlet/pallas_call | solution.py:286
  37.1 4.1 %write.1 = (f32[1,384,1536]{2,1,0:T(8,128)}, f32[1,384,1536]{2,1,0:T(8,128)}, f32[1,384,1536]{2,1,0:T(8,128)}, f32[1,384,1536]{2,1,0:T(8,128)}, f32[1,3]{1,0:T(1,128)}) custom-call(f32[12,384,128]{2,1,0:T(8,128)S(1)} %get-tuple-element.15.w1, f32[12,384,128]{2,1,0:T(8,128)S(1)} %get-tuple-element.16.w2, f32[12,384,128]{2,1,0:T(8,128)S(1)} %get-tuple-element.17.w3, ...), custom_call_target="tpu_custom_call" | custom-call | tf_op jit(solution)/shard_map/write/pallas_call | solution.py:313

commit v3 on v2

--- a/solution.py
+++ b/solution.py
@@ -19,6 +19,7 @@
 TOP, BOT = OFF, OFF + R
 ROWS = R + 2 * OFF
 EDGE = 16
+UNROLL = 6
 PIXELS = float(NROW * NCOL * R * C)
 
 
@@ -68,14 +69,16 @@
             acc = block(r, TOP <= r < BOT, acc)
         return acc
     n = len(rows)
-    u = next(q for q in (6, 4, 3, 2, 1) if n % q == 0)
 
     def several(i, acc):
-        for j in range(u):
-            acc = block(pl.multiple_of(rows[0] + 8 * (i * u + j), 8), True, acc)
+        for j in range(UNROLL):
+            acc = block(pl.multiple_of(rows[0] + 8 * (i * UNROLL + j), 8), True, acc)
         return acc
 
-    return lax.fori_loop(0, n // u, several, acc)
+    acc = lax.fori_loop(0, n // UNROLL, several, acc)
+    for r in rows[n - n % UNROLL:]:
+        acc = block(r, True, acc)
+    return acc
 
 
 def kernel_main(
@@ -168,48 +171,54 @@
     rim = (NCH - 1, HALO, 0)
     rim_own = (NCH - 1, 0)
 
+    every = tuple(range(NCH + 1))
     mid1, mid2, mid3 = (range(TOP + k, BOT - k, 8) for k in (8, 16, 24))
-    a1 = stage(c0, c1, 0, 1, mid1, whole, w1, inner)
-    a2 = stage(c1, c2, 0, 2, mid2, whole, w2, inner)
-    a3 = stage(c2, smooth, OFF, 4, mid3, inner, w3, inner)
-
-    for k in range(8):
-        _, dr, dc, _, _ = halos[k]
-        arrives = {0: right, 1: left, 2: down, 3: up,
-                   4: both(down, right), 5: both(down, left),
-                   6: both(up, right), 7: both(up, left)}[k]
-
-        @pl.when(arrives)
+
+    arrives = (right, left, down, up,
+               both(down, right), both(down, left), both(up, right), both(up, left))
+
+    def wait_halo(k):
+        @pl.when(arrives[k])
         def _():
             halo_copy(k).wait_recv()
 
-    lane = lax.broadcasted_iota(jnp.int32, (8, 128), 1)
     src_lane = lax.broadcasted_iota(jnp.int32, (128, 128), 0)
     dst_lane = lax.broadcasted_iota(jnp.int32, (128, 128), 1)
 
-    def mirrored(chunk, total, dst):
-        turn = (src_lane + dst_lane == total).astype(F32)
-        dst[pl.ds(8, ROWS - 16), :] = lax.dot_general(
-            c0[chunk, pl.ds(8, ROWS - 16), :], turn, (((1,), (0,)), ((), ())),
-            precision=lax.Precision.HIGHEST, preferred_element_type=F32,
-        )
-
-    @pl.when(jnp.logical_not(left))
-    def _():
-        mirrored(0, 128, from_left)
-
-    @pl.when(jnp.logical_not(right))
-    def _():
-        mirrored(NCH - 1, 126, from_right)
-
-    def merge(i, carry):
-        r = pl.multiple_of(8 + 8 * i, 8)
-        c0[HALO, pl.ds(r, 8), :] = jnp.where(
-            lane < 64, from_right[pl.ds(r, 8), :], from_left[pl.ds(r, 8), :]
-        )
-        return carry
-
-    lax.fori_loop(0, (ROWS - 16) // 8, merge, 0)
+    def halo_chunk(spans):
+        def mirrored(chunk, total, dst):
+            turn = (src_lane + dst_lane == total).astype(F32)
+            for span in spans:
+                dst[span, :] = lax.dot_general(
+                    c0[chunk, span, :], turn, (((1,), (0,)), ((), ())),
+                    precision=lax.Precision.HIGHEST, preferred_element_type=F32,
+                )
+
+        @pl.when(jnp.logical_not(left))
+        def _():
+            mirrored(0, 128, from_left)
+
+        @pl.when(jnp.logical_not(right))
+        def _():
+            mirrored(NCH - 1, 126, from_right)
+
+        for span in spans:
+            c0[HALO, span, :] = jnp.where(
+                lax.broadcasted_iota(jnp.int32, (span.size, 128), 1) < 64,
+                from_right[span, :], from_left[span, :],
+            )
+
+    a1 = stage(c0, c1, 0, 1, mid1, inner, w1, inner)
+    wait_halo(0)
+    wait_halo(1)
+    halo_chunk([own])
+    a1 += stage(c0, c1, 0, 1, mid1, rim, w1, rim_own)
+    a2 = stage(c1, c2, 0, 2, mid2, every, w2, whole)
+    a3 = stage(c2, smooth, OFF, 4, mid3, whole, w3, whole)
+
+    for k in range(2, 8):
+        wait_halo(k)
+    halo_chunk([above, below])
 
     @pl.when(jnp.logical_not(up))
     def _():
@@ -220,11 +229,6 @@
     def _():
         for i in range(1, 15):
             c0[:, pl.ds(BOT - 1 + i, 1), :] = c0[:, pl.ds(BOT - 1 - i, 1), :]
-
-    every = tuple(range(NCH + 1))
-    a1 += stage(c0, c1, 0, 1, mid1, rim, w1, rim_own)
-    a2 += stage(c1, c2, 0, 2, mid2, rim, w2, rim_own)
-    a3 += stage(c2, smooth, OFF, 4, mid3, rim_own, w3, rim_own)
 
     def ends(a, b):
         return list(range(TOP + a, TOP + b, 8)) + list(range(BOT - b, BOT - a, 8))

time: 41.3 us -> 37.2 us (0.901)
  Pallas kernels: 40.6 us -> 36.5 us
    pallas_call x1, Pallas kernels: 36.5 us -> 32.4 us  [on_device(): pl.pallas_call(kernel_main, out_shape=[block] * 4 + [jax.ShapeDtypeStruct...]
where the time goes in v3:
time: 37.2 us; the launch traced here: 37.1 us
  Pallas kernels  36.5 us (98%)
  between operations  0.64 us (2%)
    pallas_call x1, Pallas kernels, on_device(): pl.pallas_call(kernel_main, out_shape=[block] * 4 + [jax.ShapeDtypeStruct...  32.4 us
    pallas_call x1, Pallas kernels, on_device(): pl.pallas_call(kernel_write, out_shape=[out] * 4 + [jax.ShapeDtypeStruct(...  4.11 us

profile of v3, /device:TPU:1, one launch (start us, length us, event | category | flops | bytes accessed | tf_op | source)
XLA Modules:
  0.0 37.1 jit_solution(3116236486625742349)
XLA Ops:
  0.6 32.4 %starlet.1 = (f32[12,384,128]{2,1,0:T(8,128)S(1)}, f32[12,384,128]{2,1,0:T(8,128)S(1)}, f32[12,384,128]{2,1,0:T(8,128)S(1)}, f32[12,384,128]{2,1,0:T(8,128)S(1)}, f32[1,128]{1,0:T(1,128)S(1)}) custom-call(f32[1,384,1536]{2,1,0:T(8,128)} %cube.1), custom_call_target="tpu_custom_call" | custom-call | tf_op jit(solution)/shard_map/starlet/pallas_call | solution.py:290
  33.0 4.1 %write.1 = (f32[1,384,1536]{2,1,0:T(8,128)}, f32[1,384,1536]{2,1,0:T(8,128)}, f32[1,384,1536]{2,1,0:T(8,128)}, f32[1,384,1536]{2,1,0:T(8,128)}, f32[1,3]{1,0:T(1,128)}) custom-call(f32[12,384,128]{2,1,0:T(8,128)S(1)} %get-tuple-element.15.w1, f32[12,384,128]{2,1,0:T(8,128)S(1)} %get-tuple-element.16.w2, f32[12,384,128]{2,1,0:T(8,128)S(1)} %get-tuple-element.17.w3, ...), custom_call_target="tpu_custom_call" | custom-call | tf_op jit(solution)/shard_map/write/pallas_call | solution.py:317

commit v4 on v3

--- a/solution.py
+++ b/solution.py
@@ -125,33 +125,37 @@
             load_sem.at[c, part],
         )
 
+    barrier = pltpu.get_barrier_semaphore()
+    count = jnp.int32(NX * NCOL - 1 + NZ - 1)
+    for exists, dr, dc, _, _ in halos:
+        count = count + exists.astype(jnp.int32)
+
+        @pl.when(exists)
+        def _():
+            pl.semaphore_signal(barrier, inc=1, device_id=(row + dr, col + dc), device_id_type=MESH)
+
+    plane_order = [(dx, dc) for dx in range(NX) for dc in range(NCOL) if dx or dc]
+    plane_order.sort(key=lambda p: -(min(p[0], NX - p[0]) + min(p[1] // 2, NCOL // 2 - p[1] // 2)))
+    line_order = sorted(range(1, NZ), key=lambda k: -min(k, NZ - k))
+
+    def plane_peer(k):
+        dx, dc = k
+        return (((x + dx) % NX) * NZ + z, (col + dc) % NCOL)
+
+    def line_peer(k):
+        return (x * NZ + (z + k) % NZ, col)
+
+    for k in plane_order:
+        pl.semaphore_signal(barrier, inc=1, device_id=plane_peer(k), device_id_type=MESH)
+    for k in line_order:
+        pl.semaphore_signal(barrier, inc=1, device_id=line_peer(k), device_id_type=MESH)
+
     order = [0, NCH - 1] + list(range(1, NCH - 1))
     for c in order:
         load(c, 0).start()
         load(c, 1).start()
     for c in order:
         load(c, 2).start()
-
-    barrier = pltpu.get_barrier_semaphore()
-    count = jnp.int32(NX * NCOL - 1 + NZ - 1)
-    for exists, dr, dc, _, _ in halos:
-        count = count + exists.astype(jnp.int32)
-
-        @pl.when(exists)
-        def _():
-            pl.semaphore_signal(barrier, inc=1, device_id=(row + dr, col + dc), device_id_type=MESH)
-
-    def plane_peer(k):
-        other = (me_plane + k) % (NX * NCOL)
-        return ((other // NCOL) * NZ + z, other % NCOL)
-
-    def line_peer(k):
-        return (x * NZ + (z + k) % NZ, col)
-
-    for k in range(1, NX * NCOL):
-        pl.semaphore_signal(barrier, inc=1, device_id=plane_peer(k), device_id_type=MESH)
-    for k in range(1, NZ):
-        pl.semaphore_signal(barrier, inc=1, device_id=line_peer(k), device_id_type=MESH)
 
     for c in order:
         load(c, 0).wait()
@@ -208,12 +212,16 @@
                 from_right[span, :], from_left[span, :],
             )
 
+    inner2 = tuple(range(2, NCH - 2))
+    rim2 = (NCH - 2, NCH - 1, HALO, 0, 1)
+    rim2_own = (NCH - 2, NCH - 1, 0, 1)
     a1 = stage(c0, c1, 0, 1, mid1, inner, w1, inner)
+    a2 = stage(c1, c2, 0, 2, mid2, inner2, w2, inner2)
     wait_halo(0)
     wait_halo(1)
     halo_chunk([own])
     a1 += stage(c0, c1, 0, 1, mid1, rim, w1, rim_own)
-    a2 = stage(c1, c2, 0, 2, mid2, every, w2, whole)
+    a2 += stage(c1, c2, 0, 2, mid2, rim2, w2, rim2_own)
     a3 = stage(c2, smooth, OFF, 4, mid3, whole, w3, whole)
 
     for k in range(2, 8):
@@ -244,10 +252,10 @@
 
     vec = jnp.where(lane1 == 0, total(a1), jnp.where(lane1 == 1, total(a2), total(a3)))
 
-    def gather(value, own_ref, slots, index, count, peer, which):
+    def gather(value, own_ref, slots, index, count, peer, steps, which):
         own_ref[...] = value
         slots[pl.ds(index, 1)] = value[None]
-        for k in range(1, count):
+        for k in steps:
             pltpu.make_async_remote_copy(
                 src_ref=own_ref, dst_ref=slots.at[index],
                 send_sem=sum_send.at[which], recv_sem=sum_recv.at[which],
@@ -257,8 +265,8 @@
         pltpu.make_async_copy(arrived, arrived, sum_recv.at[which]).wait()
         return jnp.sum(slots[...], axis=0)
 
-    vec = gather(vec, mine, plane_sums, me_plane, NX * NCOL, plane_peer, 0)
-    vec = gather(vec, mine2, line_sums, z, NZ, line_peer, 1)
+    vec = gather(vec, mine, plane_sums, me_plane, NX * NCOL, plane_peer, plane_order, 0)
+    vec = gather(vec, mine2, line_sums, z, NZ, line_peer, line_order, 1)
     sigma[...] = jnp.sqrt(vec * (1.0 / PIXELS) + 1e-6)
 
     for which, slots, count in ((0, plane_sums, NX * NCOL), (1, line_sums, NZ)):

time: 37.2 us -> 36.1 us (0.970)
  Pallas kernels: 36.5 us -> 35.4 us
    pallas_call x1, Pallas kernels: 32.4 us -> 31.3 us  [on_device(): pl.pallas_call(kernel_main, out_shape=[block] * 4 + [jax.ShapeDtypeStruct...]
where the time goes in v4:
time: 36.1 us; the launch traced here: 36 us
  Pallas kernels  35.4 us (98%)
  between operations  0.64 us (2%)
    pallas_call x1, Pallas kernels, on_device(): pl.pallas_call(kernel_main, out_shape=[block] * 4 + [jax.ShapeDtypeStruct...  31.3 us
    pallas_call x1, Pallas kernels, on_device(): pl.pallas_call(kernel_write, out_shape=[out] * 4 + [jax.ShapeDtypeStruct(...  4.11 us

profile of v4, /device:TPU:1, one launch (start us, length us, event | category | flops | bytes accessed | tf_op | source)
XLA Modules:
  0.0 36.0 jit_solution(3349797291029410898)
XLA Ops:
  0.6 31.3 %starlet.1 = (f32[12,384,128]{2,1,0:T(8,128)S(1)}, f32[12,384,128]{2,1,0:T(8,128)S(1)}, f32[12,384,128]{2,1,0:T(8,128)S(1)}, f32[12,384,128]{2,1,0:T(8,128)S(1)}, f32[1,128]{1,0:T(1,128)S(1)}) custom-call(f32[1,384,1536]{2,1,0:T(8,128)} %cube.1), custom_call_target="tpu_custom_call" | custom-call | tf_op jit(solution)/shard_map/starlet/pallas_call | solution.py:298
  31.9 4.1 %write.1 = (f32[1,384,1536]{2,1,0:T(8,128)}, f32[1,384,1536]{2,1,0:T(8,128)}, f32[1,384,1536]{2,1,0:T(8,128)}, f32[1,384,1536]{2,1,0:T(8,128)}, f32[1,3]{1,0:T(1,128)}) custom-call(f32[12,384,128]{2,1,0:T(8,128)S(1)} %get-tuple-element.15.w1, f32[12,384,128]{2,1,0:T(8,128)S(1)} %get-tuple-element.16.w2, f32[12,384,128]{2,1,0:T(8,128)S(1)} %get-tuple-element.17.w3, ...), custom_call_target="tpu_custom_call" | custom-call | tf_op jit(solution)/shard_map/write/pallas_call | solution.py:325

commit v5 on v4

--- a/solution.py
+++ b/solution.py
@@ -19,7 +19,7 @@
 TOP, BOT = OFF, OFF + R
 ROWS = R + 2 * OFF
 EDGE = 16
-UNROLL = 6
+CUT = 8 * ((R // 8 - 2) // 2) + 16
 PIXELS = float(NROW * NCOL * R * C)
 
 
@@ -69,16 +69,14 @@
             acc = block(r, TOP <= r < BOT, acc)
         return acc
     n = len(rows)
+    u = n // 2 if n % 2 == 0 else n
 
     def several(i, acc):
-        for j in range(UNROLL):
-            acc = block(pl.multiple_of(rows[0] + 8 * (i * UNROLL + j), 8), True, acc)
+        for j in range(u):
+            acc = block(pl.multiple_of(rows[0] + 8 * (i * u + j), 8), True, acc)
         return acc
 
-    acc = lax.fori_loop(0, n // UNROLL, several, acc)
-    for r in rows[n - n % UNROLL:]:
-        acc = block(r, True, acc)
-    return acc
+    return lax.fori_loop(0, n // u, several, acc)
 
 
 def kernel_main(
@@ -118,7 +116,7 @@
         )
 
     def load(c, part):
-        a, n = ((0, EDGE), (R - EDGE, EDGE), (EDGE, R - 2 * EDGE))[part]
+        a, n = ((0, EDGE), (R - EDGE, EDGE), (EDGE, CUT - EDGE), (CUT, R - EDGE - CUT))[part]
         return pltpu.make_async_copy(
             cube.at[0, pl.ds(a, n), pl.ds(c * 128, 128)],
             c0.at[c, pl.ds(TOP + a, n)],
@@ -154,22 +152,24 @@
     for c in order:
         load(c, 0).start()
         load(c, 1).start()
-    for c in order:
+    for c in order[:2]:
         load(c, 2).start()
+        load(c, 3).start()
+    for part in (2, 3):
+        for c in order[2:]:
+            load(c, part).start()
 
     for c in order:
         load(c, 0).wait()
         load(c, 1).wait()
-    load(0, 2).wait()
-    load(NCH - 1, 2).wait()
+    for c in order[:2]:
+        load(c, 2).wait()
+        load(c, 3).wait()
     pl.semaphore_wait(barrier, count)
     for k in range(8):
         @pl.when(halos[k][0])
         def _():
             halo_copy(k).start()
-    for c in order[2:]:
-        load(c, 2).wait()
-
     inner = tuple(range(1, NCH - 1))
     whole = tuple(range(NCH))
     rim = (NCH - 1, HALO, 0)
@@ -215,7 +215,13 @@
     inner2 = tuple(range(2, NCH - 2))
     rim2 = (NCH - 2, NCH - 1, HALO, 0, 1)
     rim2_own = (NCH - 2, NCH - 1, 0, 1)
-    a1 = stage(c0, c1, 0, 1, mid1, inner, w1, inner)
+    half = len(mid1) // 2
+    for c in order[2:]:
+        load(c, 2).wait()
+    a1 = stage(c0, c1, 0, 1, mid1[:half], inner, w1, inner)
+    for c in order[2:]:
+        load(c, 3).wait()
+    a1 += stage(c0, c1, 0, 1, mid1[half:], inner, w1, inner)
     a2 = stage(c1, c2, 0, 2, mid2, inner2, w2, inner2)
     wait_halo(0)
     wait_halo(1)
@@ -310,7 +316,7 @@
             pltpu.VMEM((1, 128), F32),
             pltpu.VMEM((NX * NCOL, 1, 128), F32),
             pltpu.VMEM((NZ, 1, 128), F32),
-            pltpu.SemaphoreType.DMA((NCH, 3)),
+            pltpu.SemaphoreType.DMA((NCH, 4)),
             pltpu.SemaphoreType.DMA((8,)),
             pltpu.SemaphoreType.DMA((8,)),
             pltpu.SemaphoreType.DMA((2,)),

time: 36.1 us -> 34.2 us (0.947)
  Pallas kernels: 35.4 us -> 33.4 us
    pallas_call x1, Pallas kernels: 31.3 us -> 29.3 us  [on_device(): pl.pallas_call(kernel_main, out_shape=[block] * 4 + [jax.ShapeDtypeStruct...]
where the time goes in v5:
time: 34.2 us; the launch traced here: 34.1 us
  Pallas kernels  33.4 us (98%)
  between operations  0.64 us (2%)
    pallas_call x1, Pallas kernels, on_device(): pl.pallas_call(kernel_main, out_shape=[block] * 4 + [jax.ShapeDtypeStruct...  29.3 us
    pallas_call x1, Pallas kernels, on_device(): pl.pallas_call(kernel_write, out_shape=[out] * 4 + [jax.ShapeDtypeStruct(...  4.11 us

profile of v5, /device:TPU:1, one launch (start us, length us, event | category | flops | bytes accessed | tf_op | source)
XLA Modules:
  0.0 34.1 jit_solution(14038414755273212674)
XLA Ops:
  0.6 29.3 %starlet.1 = (f32[12,384,128]{2,1,0:T(8,128)S(1)}, f32[12,384,128]{2,1,0:T(8,128)S(1)}, f32[12,384,128]{2,1,0:T(8,128)S(1)}, f32[12,384,128]{2,1,0:T(8,128)S(1)}, f32[1,128]{1,0:T(1,128)S(1)}) custom-call(f32[1,384,1536]{2,1,0:T(8,128)} %cube.1), custom_call_target="tpu_custom_call" | custom-call | tf_op jit(solution)/shard_map/starlet/pallas_call | solution.py:304
  30.0 4.1 %write.1 = (f32[1,384,1536]{2,1,0:T(8,128)}, f32[1,384,1536]{2,1,0:T(8,128)}, f32[1,384,1536]{2,1,0:T(8,128)}, f32[1,384,1536]{2,1,0:T(8,128)}, f32[1,3]{1,0:T(1,128)}) custom-call(f32[12,384,128]{2,1,0:T(8,128)S(1)} %get-tuple-element.15.w1, f32[12,384,128]{2,1,0:T(8,128)S(1)} %get-tuple-element.16.w2, f32[12,384,128]{2,1,0:T(8,128)S(1)} %get-tuple-element.17.w3, ...), custom_call_target="tpu_custom_call" | custom-call | tf_op jit(solution)/shard_map/write/pallas_call | solution.py:331
